TPU v7x, 32 devices: a whole 2x2x4 slice. The times are simulated.
32 devices in a mesh: light: 4 (over y, x), screen: 8 (over z, core).
Axes of the slice: x: 2, y: 2, z: 4, core: 2. Of those that a mesh axis runs over, the one named last changes fastest.
Arguments:
- density: float32 [128, 256, 512], P('screen', None, 'light'), may hold values from 0 to 1.09375, as said below
- albedo: float32 [128, 256, 512], P('screen', None, 'light'), may hold values from 0.2 to 1
- light_in: float32 [128, 256], replicated, may hold values from 0.5 to 1.5
- occupancy: int32 [8, 16, 32], P('screen', None, 'light'), may hold values 0 or 1
- phase: int32 [256, 512], replicated, may hold values from 0 to 15
- fractions: float32 [3, 16], replicated, may hold values from 0 to 1
Outputs:
- image: float32 [256, 512], P('screen', 'light')
- transmittance: float32 [256, 512], P('screen', 'light')
- lit_bricks: float32 [128, 256, 512], P('light', 'screen')
Inputs may be any that keep to these rules, and one draw needn't show every extreme that they name: `density`: nonnegative extinction of each cell. `occupancy`: 1 where the brick of 16 cells on a side is occupied.
All inputs are finite; a program needn't handle non-finite values. No bound on the sum of `occupancy` on one device may be relied on, other than what follows from the above.
Results may differ from a plain program's by a relative error of at most 0.0003.
Values sent between devices are 32-bit elements; how exact they have to be, the bound alone decides.
No kernel may reach another device: no remote copies, remote signals or barrier semaphores. Data moves between devices by JAX's collectives and lax.ppermute only.
A program may use at most 192 MiB of HBM per device.

v0:
```python
import jax
import jax.numpy as jnp
from jax import lax
from jax.sharding import PartitionSpec as P

BRICK = 16


def passed_along(value, axis, by):
    peers = lax.axis_size(axis)
    pairs = [(i, i + by) for i in range(peers) if 0 <= i + by < peers]
    return lax.ppermute(value, axis, pairs)


def carried_in(part, axis, combine, identity):
    place = lax.axis_index(axis)
    gathered = lax.all_gather(part, axis)
    state = jnp.zeros_like(part) + jnp.asarray(identity, part.dtype)

    def one(step, state):
        return combine(state, lax.dynamic_index_in_dim(gathered, step, 0, False))

    return lax.fori_loop(0, place, one, state)


def prefix_last(values):
    length = values.shape[-1]
    block = 128
    count = length // block
    shaped = values.reshape(values.shape[:-1] + (count, block))
    rowsidx = lax.broadcasted_iota(jnp.int32, (block, block), 0)
    colsidx = lax.broadcasted_iota(jnp.int32, (block, block), 1)
    upper = (rowsidx < colsidx).astype(jnp.float32)
    within = jnp.matmul(shaped, upper, precision=lax.Precision.HIGHEST)
    totals = jnp.sum(shaped, axis=-1)
    carried = jnp.cumsum(totals, axis=-1) - totals
    return (within + carried[..., None]).reshape(values.shape)


def prefix_first(values):
    length = values.shape[0]
    count = length // length
    shaped = values.reshape(count, length, -1)
    rowsidx = lax.broadcasted_iota(jnp.int32, (length, length), 0)
    colsidx = lax.broadcasted_iota(jnp.int32, (length, length), 1)
    lower = (colsidx < rowsidx).astype(jnp.float32)
    within = jnp.einsum("ij,bjr->bir", lower, shaped, precision=lax.Precision.HIGHEST)
    totals = jnp.sum(shaped, axis=1)
    carried = jnp.cumsum(totals, axis=0) - totals
    return (within + carried[:, None]).reshape(values.shape)


def corner_fractions(rays, fractions):
    levels = lax.broadcasted_iota(jnp.int32, (fractions.shape[1], 1, 1), 0)
    onehot = (rays[None] == levels).astype(jnp.float32)
    return jnp.einsum("kp,prc->krc", fractions, onehot, precision=lax.Precision.HIGHEST)


def resample(field, tail, weights, deep, cols):
    first = field[:, 0:cols]
    second = field[:, 1 : cols + 1]
    edge_first = tail[:, 0:cols]
    edge_second = tail[:, 1 : cols + 1]
    first_next = jnp.concatenate([first[:, :, 1:], edge_first], axis=2)
    second_next = jnp.concatenate([second[:, :, 1:], edge_second], axis=2)
    depth_w = weights[0]
    column_w = weights[1]
    light_w = weights[2]
    near = first + column_w * (second - first)
    further = first_next + column_w * (second_next - first_next)
    mixed = near + light_w * (further - near)
    lower = mixed[0:deep]
    higher = mixed[1 : deep + 1]
    return lower + depth_w * (higher - lower)


def composite(extinct, shaded):
    screened = prefix_first(extinct)
    part = jnp.sum(jnp.exp(-screened) * (1.0 - jnp.exp(-extinct)) * shaded, axis=0)
    return (part, jnp.sum(extinct, axis=0))


def finish(parts, totals):
    before = jnp.cumsum(totals, axis=0) - totals
    picture = jnp.sum(jnp.exp(-before) * parts, axis=0)
    return (picture, jnp.exp(-jnp.sum(totals, axis=0)))


def march_slabs(masked, lit, phase, fractions):
    slab_b, width_a, slab_l = masked.shape
    light_idx = lax.axis_index("light")
    rims = passed_along((masked[:2], lit[:2]), "screen", -1)
    dens_ext = jnp.pad(jnp.concatenate([masked, rims[0]], axis=0), ((0, 0), (0, 2), (0, 0)))
    lit_ext = jnp.pad(jnp.concatenate([lit, rims[1]], axis=0), ((0, 0), (0, 2), (0, 0)))
    tails = passed_along((dens_ext[:, :, :1], lit_ext[:, :, :1]), "light", -1)
    rays = lax.dynamic_slice_in_dim(phase, light_idx * slab_l, slab_l, 1)
    weights = corner_fractions(rays, fractions)
    extinct = resample(dens_ext, tails[0], weights, slab_b, width_a)
    shaded = resample(lit_ext, tails[1], weights, slab_b, width_a)
    part, total = composite(extinct, shaded)
    parts, totals = (
        lax.all_to_all(part[None], "screen", split_axis=1, concat_axis=0, tiled=True),
        lax.all_to_all(total[None], "screen", split_axis=1, concat_axis=0, tiled=True),
    )
    return finish(parts, totals)


def local(density, albedo, light_in, occupancy, phase, fractions):
    slab_b, width_a, slab_l = density.shape
    bricks_b, bricks_a, bricks_l = occupancy.shape
    masked = (
        density.reshape(bricks_b, BRICK, bricks_a, BRICK, bricks_l, BRICK)
        * occupancy.astype(jnp.float32)[:, None, :, None, :, None]
    ).reshape(density.shape)
    screen_idx = lax.axis_index("screen")
    local_depth = prefix_last(masked)
    totals = jnp.sum(masked, axis=2)
    before = carried_in(totals, "light", jnp.add, jnp.zeros_like(totals))
    incoming = lax.dynamic_slice_in_dim(light_in, screen_idx * slab_b, slab_b, 0)
    lit = albedo * incoming[:, :, None] * jnp.exp(-(local_depth + before[:, :, None]))
    lit_cam = lax.all_to_all(lit, "screen", split_axis=1, concat_axis=0, tiled=True)
    lit_cam = lax.all_to_all(lit_cam, "light", split_axis=0, concat_axis=2, tiled=True)
    picture, passing = march_slabs(masked, lit, phase, fractions)
    return (picture, passing, lit_cam)


def solution(mesh):
    return jax.shard_map(
        local,
        mesh=mesh,
        in_specs=(
            P("screen", None, "light"),
            P("screen", None, "light"),
            P(),
            P("screen", None, "light"),
            P(),
            P(),
        ),
        out_specs=(P("screen", "light"), P("screen", "light"), P("light", "screen", None)),
        check_vma=False,
    )
```

profile of v0, /device:TPU:0, one launch (start us, length us, event | category | flops | bytes accessed | tf_op | source)
XLA Modules:
  0.0 195.5 jit_solution(17380704200879934052)
XLA Ops:
  0.7 0.7 convert_bitcast_fusion
  1.9 2.2 %fusion.35 = (f32[16,256]{1,0:T(8,128)S(1)}, f32[16,256,128]{2,1,0:T(8,128)S(1)}) fusion(f32[16,256,128]{2,1,0:T(8,128)} %param.8, f32[256,128]{1,0:T(8,128)S(1)} %mul.121), kind=kLoop, calls=%fused_computation.62 | loop fusion | flops 1044480 | bytes 4341760 | tf_op jit(solution)/shard_map/reduce_sum | solution.py:35
  4.2 9.7 %all-gather = f32[64,256]{1,0:T(8,128)S(1)} all-gather(f32[16,256]{1,0:T(8,128)S(1)} %get-tuple-element.35), channel_id=2, replica_groups=mesh['light'=4,'screen'=8] {'light'}, dimensions={0}, use_global_device_ids=true | all-gather | bytes 81920 | tf_op jit(solution)/shard_map/all_gather | solution.py:17
  13.9 0.7 constant_dynamic-slice_fusion
  14.6 3.8 %exponential_multiply_fusion = f32[16,256,128]{2,1,0:T(8,128)S(1)} fusion(f32[16,256,128]{2,1,0:T(8,128)} %param.9, f32[16,256,128]{2,1,0:T(8,128)S(1)} %get-tuple-element.36, f32[16,256]{1,0:T(8,128)S(1)} %get-tuple-element.26, f32[16,256]{1,0:T(8,128)S(1)} %sub.66, f32[16,256]{1,0:T(8,128)S(1)} %constant_dynamic-slice_fusion), kind=kOutput, calls=%fused_computation.42 | convolution fusion | flops 807944192 | bytes 6340608 | tf_op jit(solution)/shard_map/dot_general | solution.py:34
  18.5 1.3 copy-done.3
  19.8 1.3 collective-permute-start.2
  21.1 10.6 %reshape.82 = f32[1,16,16,16,8,16]{5,4,3,2,1,0:T(8,128)} reshape(f32[16,256,128]{2,1,0:T(8,128)} %param.8) | data formatting | bytes 4194304 | tf_op jit(solution)/shard_map/reshape | solution.py:112
  31.7 1.9 slice_multiply_fusion
  33.6 1.3 slice.74
  34.8 1.3 collective-permute-start
  36.2 0.7 fusion.27
  36.9 1.0 fusion.38
  37.9 1.7 pad_maximum_fusion.1
  39.6 2.1 %pad_slice_fusion.2 = f32[18,256,127]{2,1,0:T(8,128)} fusion(f32[18,256,128]{2,1,0:T(8,128)S(1)} %pad_maximum_fusion.1), kind=kLoop, calls=%fused_computation.25 | loop fusion | bytes 4700160 | tf_op jit(solution)/shard_map/slice | solution.py:65
  41.7 1.6 pad_slice_fusion.3
  43.4 0.9 copy-done.6
  44.4 2.2 %pad_slice_fusion.4 = f32[18,256,127]{2,1,0:T(8,128)} fusion(f32[18,256,128]{2,1,0:T(8,128)S(1)} %pad_maximum_fusion), kind=kLoop, calls=%fused_computation.27 | loop fusion | bytes 4700160 | tf_op jit(solution)/shard_map/slice | solution.py:65
  46.6 1.6 pad_slice_fusion.5
  48.2 2.7 %copy.33 = f32[18,258,1]{1,2,0:T(1,128)S(1)} copy(f32[18,258,1]{2,1,0:T(8,128)} %pad_slice_fusion.3) | data formatting | bytes 37152 | tf_op jit(solution)/shard_map/slice | solution.py:95
  50.9 1.3 collective-permute-start.3
  52.2 2.7 %copy.30 = f32[18,258,1]{1,2,0:T(1,128)S(1)} copy(f32[18,258,1]{2,1,0:T(8,128)} %pad_slice_fusion.5) | data formatting | bytes 37152 | tf_op jit(solution)/shard_map/slice | solution.py:95
  54.9 1.6 collective-permute-start.1
  56.5 3.7 %fusion.3 = f32[18,256,127]{2,1,0:T(8,128)} fusion(f32[2,256,128]{2,1,0:T(8,128)S(1)} %collective-permute-done.2, f32[16,256,128]{2,1,0:T(8,128)} %copy-done.3), kind=kLoop, calls=%fused_computation.9 | loop fusion | flops 585216 | bytes 4700160 | tf_op jit(solution)/shard_map/concatenate | solution.py:94
  60.2 2.1 %fusion.4 = f32[18,256,127]{2,1,0:T(8,128)} fusion(f32[2,256,128]{2,1,0:T(8,128)S(1)} %collective-permute-done, f32[16,256,128]{2,1,0:T(8,128)S(1)} %copy-done.7), kind=kLoop, calls=%fused_computation.10 | loop fusion | flops 585216 | bytes 4700160 | tf_op jit(solution)/shard_map/concatenate | solution.py:93
  62.4 2.1 %copy.35 = f32[18,256,1]{2,1,0:T(8,128)} copy(f32[18,256,1]{1,2,0:T(1,128)S(1)} %get-tuple-element.44) | data formatting | bytes 36864 | tf_op jit(solution)/shard_map/slice | solution.py:63
  64.6 2.2 %copy.34 = f32[18,256,1]{2,1,0:T(8,128)} copy(f32[18,256,1]{1,2,0:T(1,128)S(1)} %get-tuple-element.45) | data formatting | bytes 36864 | tf_op jit(solution)/shard_map/slice | solution.py:62
  66.8 2.1 %copy.32 = f32[18,256,1]{2,1,0:T(8,128)} copy(f32[18,256,1]{1,2,0:T(1,128)S(1)} %get-tuple-element.46) | data formatting | bytes 36864 | tf_op jit(solution)/shard_map/slice | solution.py:63
  69.0 2.1 %copy.31 = f32[18,256,1]{2,1,0:T(8,128)} copy(f32[18,256,1]{1,2,0:T(1,128)S(1)} %get-tuple-element.47) | data formatting | bytes 36864 | tf_op jit(solution)/shard_map/slice | solution.py:62
  71.1 12.0 %fusion.14 = (f32[18,256,128]{2,1,0:T(8,128)}, f32[18,256,128]{2,1,0:T(8,128)S(1)}) fusion(f32[18,256,1]{2,1,0:T(8,128)} %copy.34, f32[18,256,127]{2,1,0:T(8,128)} %fusion.3, f32[18,256,1]{2,1,0:T(8,128)} %copy.35, f32[18,256,127]{2,1,0:T(8,128)} %pad_slice_fusion.2, f32[18,256,128]{2,1,0:T(8,128)S(1)} %pad_maximum_fusion.1, f32[256,128]{1,0:T(8,128)S(1)} %bitcast.74, ...), kind=kLoop, calls=%fused_computation.24 | loop fusion | flops 12976128 | bytes 19136512 | tf_op jit(solution)/shard_map/add | solution.py:71
  83.2 2.3 %fusion.36 = (f32[256,128]{1,0:T(8,128)}, f32[16,256,128]{2,1,0:T(8,128)}) fusion(f32[18,256,128]{2,1,0:T(8,128)S(1)} %get-tuple-element.43, f32[256,128]{1,0:T(8,128)S(1)} %bitcast.72), kind=kLoop, calls=%fused_computation.63 | loop fusion | flops 2064384 | bytes 6553600 | tf_op jit(solution)/shard_map/reduce_sum | solution.py:80
  85.5 6.7 %all-to-all-start = ((f32[1,256,128]{2,0,1:T(1,128)}), f32[1,256,128]{2,0,1:T(1,128)S(1)}, u32[]{:S(2)}, u32[]{:S(2)}) async-start(f32[1,256,128]{2,0,1:T(1,128)} %bitcast.7), calls=%async_computation | async-start | bytes 262144 | tf_op jit(solution)/shard_map/all_to_all | solution.py:103
  92.2 2.5 %copy.36 = f32[16,256,128]{2,0,1:T(8,128)} copy(f32[16,256,128]{2,1,0:T(8,128)S(1)} %copy-done.4) | data formatting | bytes 4194304 | tf_op jit(solution)/shard_map/mul | solution.py:120
  94.7 4.2 %all-to-all-done = f32[1,256,128]{2,0,1:T(1,128)S(1)} async-done(((f32[1,256,128]{2,0,1:T(1,128)}), f32[1,256,128]{2,0,1:T(1,128)S(1)}, u32[]{:S(2)}, u32[]{:S(2)}) %all-to-all-start) | async-done | bytes 131104 | tf_op jit(solution)/shard_map/all_to_all | solution.py:103
  98.9 4.4 %all-to-all-start.2 = ((f32[16,256,128]{2,0,1:T(8,128)}), f32[16,256,128]{2,0,1:T(8,128)}, u32[]{:S(2)}, u32[]{:S(2)}) async-start(f32[16,256,128]{2,0,1:T(8,128)} %copy.36), calls=%async_computation.2 | async-start | bytes 4194304 | tf_op jit(solution)/shard_map/all_to_all | solution.py:121
  103.3 0.9 subtract_bitcast_fusion
  104.2 2.5 %fusion.24 = f32[2,8,256,128]{3,1,2,0:T(8,128)S(1)} fusion(f32[2,8,256,128]{3,2,1,0:T(8,128)S(1)} %bitcast.67, f32[32768]{0:T(1024)S(1)} %subtract_bitcast_fusion), kind=kOutput, calls=%fused_computation.45 | convolution fusion | flops 101712128 | bytes 4325376 | tf_op jit(solution)/shard_map/ij,bjr->bir/dot_general | solution.py:47
  107.1 1.2 copy-done.9
  108.4 1.3 fusion.16
  109.7 42.7 %all-to-all-done.2 = f32[16,256,128]{2,0,1:T(8,128)} async-done(((f32[16,256,128]{2,0,1:T(8,128)}), f32[16,256,128]{2,0,1:T(8,128)}, u32[]{:S(2)}, u32[]{:S(2)}) %all-to-all-start.2) | async-done | bytes 2097184 | tf_op jit(solution)/shard_map/all_to_all | solution.py:121
  152.3 3.4 %all-to-all-start.1 = ((f32[1,256,128]{2,0,1:T(1,128)}), f32[1,256,128]{2,0,1:T(1,128)S(1)}, u32[]{:S(2)}, u32[]{:S(2)}) async-start(f32[1,256,128]{2,0,1:T(1,128)} %bitcast.14), calls=%async_computation.1 | async-start | bytes 262144 | tf_op jit(solution)/shard_map/all_to_all | solution.py:102
  155.7 3.5 %copy.38 = f32[8,16,32,128]{3,2,1,0:T(8,128)} copy(f32[8,16,32,128]{3,1,2,0:T(8,128)} %bitcast.18) | data formatting | bytes 4194304 | tf_op jit(solution)/shard_map/all_to_all | solution.py:121
  159.3 3.1 %all-to-all-done.1 = f32[1,256,128]{2,0,1:T(1,128)S(1)} async-done(((f32[1,256,128]{2,0,1:T(1,128)}), f32[1,256,128]{2,0,1:T(1,128)S(1)}, u32[]{:S(2)}, u32[]{:S(2)}) %all-to-all-start.1) | async-done | bytes 131104 | tf_op jit(solution)/shard_map/all_to_all | solution.py:102
  162.4 6.9 %all-to-all-start.3 = ((f32[128,32,128]{2,1,0:T(8,128)}), f32[128,32,128]{2,1,0:T(8,128)S(1)}, u32[]{:S(2)}, u32[]{:S(2)}) async-start(f32[128,32,128]{2,1,0:T(8,128)} %bitcast.19), calls=%async_computation.3 | async-start | bytes 4194304 | tf_op jit(solution)/shard_map/all_to_all | solution.py:122
  169.4 0.6 negate_exponential_fusion
  170.0 0.6 fusion.41
  170.6 23.3 %all-to-all-done.3 = f32[128,32,128]{2,1,0:T(8,128)S(1)} async-done(((f32[128,32,128]{2,1,0:T(8,128)}), f32[128,32,128]{2,1,0:T(8,128)S(1)}, u32[]{:S(2)}, u32[]{:S(2)}) %all-to-all-start.3) | async-done | bytes 2097184 | tf_op jit(solution)/shard_map/all_to_all | solution.py:122
  193.9 1.6 copy.51
  (40 shorter events, 1.5 us)
Async XLA Ops:
  0.6 35.5 %copy-start = (s32[256,512]{1,0:T(8,128)S(1)}, s32[256,512]{1,0:T(8,128)}, u32[]{:S(2)}) copy-start(s32[256,512]{1,0:T(8,128)} %param.12) | copy-start | bytes 1572868
  4.1 14.3 %copy-start.5 = (f32[16,256,128]{2,1,0:T(8,128)}, f32[16,256,128]{2,1,0:T(8,128)S(1)}, u32[]{:S(2)}) copy-start(f32[16,256,128]{2,1,0:T(8,128)S(1)} %get-tuple-element.36) | copy-start | bytes 6291460
  18.5 1.3 copy-start.3
  19.8 18.1 %collective-permute-start.2 = (f32[2,256,128]{2,1,0:T(8,128)S(1)}, f32[2,256,128]{2,1,0:T(8,128)S(1)}, u32[]{:S(2)}, u32[]{:S(2)}) collective-permute-start(f32[2,256,128]{2,1,0:T(8,128)S(1)} %slice.105), channel_id=1, source_target_pairs={{1,0},{2,1},{3,2},{4,3},{5,4},{6,5},{7,6},{9,8},{10,9},{11,10},{12... | collective-permute-start | bytes 786440 | tf_op jit(solution)/shard_map/ppermute | solution.py:12
  33.6 2.6 %copy-start.12 = (f32[3,16]{1,0:T(4,128)S(1)}, f32[3,16]{1,0:T(4,128)}, u32[]{:S(2)}) copy-start(f32[3,16]{1,0:T(4,128)} %param.13) | copy-start | bytes 580
  34.8 8.5 %collective-permute-start = (f32[2,256,128]{2,1,0:T(8,128)}, f32[2,256,128]{2,1,0:T(8,128)S(1)}, u32[]{:S(2)}, u32[]{:S(2)}) collective-permute-start(f32[2,256,128]{2,1,0:T(8,128)} %slice.74), channel_id=1, source_target_pairs={{1,0},{2,1},{3,2},{4,3},{5,4},{6,5},{7,6},{9,8},{10,9},{11,10},{12... | collective-permute-start | bytes 786440 | tf_op jit(solution)/shard_map/ppermute | solution.py:12
  41.7 2.5 %copy-start.6 = (f32[16,256,128]{2,1,0:T(8,128)S(1)}, f32[16,256,128]{2,1,0:T(8,128)}, u32[]{:S(2)}) copy-start(f32[16,256,128]{2,1,0:T(8,128)} %copy-done.5) | copy-start | bytes 6291460
  44.4 2.2 %copy-start.2 = (f32[18,256,128]{2,1,0:T(8,128)}, f32[18,256,128]{2,1,0:T(8,128)S(1)}, u32[]{:S(2)}) copy-start(f32[18,256,128]{2,1,0:T(8,128)S(1)} %pad_maximum_fusion) | copy-start | bytes 7077892
  50.9 11.4 %collective-permute-start.3 = (f32[18,258,1]{1,2,0:T(1,128)S(1)}, f32[18,258,1]{1,2,0:T(1,128)S(1)}, u32[]{:S(2)}, u32[]{:S(2)}) collective-permute-start(f32[18,258,1]{1,2,0:T(1,128)S(1)} %copy.33), channel_id=1, source_target_pairs={{8,0},{16,8},{24,16},{9,1},{17,9},{25,17},{10,2},{18,10},{26,18},{... | collective-permute-start | bytes 55736 | tf_op jit(solution)/shard_map/ppermute | solution.py:12
  54.9 5.3 %copy-start.7 = (f32[16,256,128]{2,1,0:T(8,128)S(1)}, f32[16,256,128]{2,1,0:T(8,128)}, u32[]{:S(2)}) copy-start(f32[16,256,128]{2,1,0:T(8,128)} %copy-done.5) | copy-start | bytes 6291460
  54.9 11.8 %collective-permute-start.1 = (f32[18,258,1]{1,2,0:T(1,128)S(1)}, f32[18,258,1]{1,2,0:T(1,128)S(1)}, u32[]{:S(2)}, u32[]{:S(2)}) collective-permute-start(f32[18,258,1]{1,2,0:T(1,128)S(1)} %copy.30), channel_id=1, source_target_pairs={{8,0},{16,8},{24,16},{9,1},{17,9},{25,17},{10,2},{18,10},{26,18},{... | collective-permute-start | bytes 55736 | tf_op jit(solution)/shard_map/ppermute | solution.py:12
  66.8 4.3 %copy-start.10 = (f32[1,256,128]{2,0,1:T(1,128)S(1)}, f32[1,256,128]{2,0,1:T(1,128)}, u32[]{:S(2)}) copy-start(f32[1,256,128]{2,0,1:T(1,128)} %get-tuple-element.40) | copy-start | bytes 393220
  66.8 4.3 %copy-start.11 = (f32[1,256,128]{2,0,1:T(1,128)S(1)}, f32[1,256,128]{2,0,1:T(1,128)}, u32[]{:S(2)}) copy-start(f32[1,256,128]{2,0,1:T(1,128)} %get-tuple-element.41) | copy-start | bytes 393220
  83.2 9.0 %copy-start.4 = (f32[16,256,128]{2,1,0:T(8,128)S(1)}, f32[16,256,128]{2,1,0:T(8,128)}, u32[]{:S(2)}) copy-start(f32[16,256,128]{2,1,0:T(8,128)} %copy-done.3) | copy-start | bytes 6291460
  85.5 13.4 %all-to-all-start = ((f32[1,256,128]{2,0,1:T(1,128)}), f32[1,256,128]{2,0,1:T(1,128)S(1)}, u32[]{:S(2)}, u32[]{:S(2)}) async-start(f32[1,256,128]{2,0,1:T(1,128)} %bitcast.7), calls=%async_computation | async-start | bytes 262144 | tf_op jit(solution)/shard_map/all_to_all | solution.py:103
  94.7 9.5 %copy-start.8 = (f32[16,256,128]{2,1,0:T(8,128)S(1)}, f32[16,256,128]{2,1,0:T(8,128)}, u32[]{:S(2)}) copy-start(f32[16,256,128]{2,1,0:T(8,128)} %get-tuple-element.38) | copy-start | bytes 6291460
  98.9 53.4 %all-to-all-start.2 = ((f32[16,256,128]{2,0,1:T(8,128)}), f32[16,256,128]{2,0,1:T(8,128)}, u32[]{:S(2)}, u32[]{:S(2)}) async-start(f32[16,256,128]{2,0,1:T(8,128)} %copy.36), calls=%async_computation.2 | async-start | bytes 4194304 | tf_op jit(solution)/shard_map/all_to_all | solution.py:121
  106.7 1.7 copy-start.9
  152.3 10.1 %all-to-all-start.1 = ((f32[1,256,128]{2,0,1:T(1,128)}), f32[1,256,128]{2,0,1:T(1,128)S(1)}, u32[]{:S(2)}, u32[]{:S(2)}) async-start(f32[1,256,128]{2,0,1:T(1,128)} %bitcast.14), calls=%async_computation.1 | async-start | bytes 262144 | tf_op jit(solution)/shard_map/all_to_all | solution.py:102
  162.4 31.5 %all-to-all-start.3 = ((f32[128,32,128]{2,1,0:T(8,128)}), f32[128,32,128]{2,1,0:T(8,128)S(1)}, u32[]{:S(2)}, u32[]{:S(2)}) async-start(f32[128,32,128]{2,1,0:T(8,128)} %bitcast.19), calls=%async_computation.3 | async-start | bytes 4194304 | tf_op jit(solution)/shard_map/all_to_all | solution.py:122
  169.4 26.2 %copy-start.1 = (s32[256,512]{1,0:T(8,128)S(1)}, s32[256,512]{1,0:T(8,128)}, u32[]{:S(2)}) copy-start(s32[256,512]{1,0:T(8,128)} %param.12) | copy-start | bytes 1572868
where the time goes:
time: 197 us; the launch traced here: 196 us
  waiting for transfers between devices  73.3 us (37%)
  local copies, waits for them, and re-layouts  47.3 us (24%)
  other arithmetic  30.4 us (15%)
  starting transfers between devices  26.8 us (14%)
  blocking collectives  9.72 us (5%)
  matrix products  7 us (4%)
    all_to_all x1, waiting for transfers between devices, local(): lax.all_to_all(lit, 'screen', split_axis=1, concat_axis=0, tiled=True)  42.7 us
    all_to_all x1, waiting for transfers between devices, local(): lax.all_to_all(lit_cam, 'light', split_axis=0, concat_axis=2, tiled=True)  23.3 us
    add x1, other arithmetic, resample(): mixed = near + light_w * (further - near)  12 us
    reshape x1, local copies, waits for them, and re-layouts, local(): density.reshape(bricks_b, BRICK, bricks_a, BRICK, bricks_l, BRICK)  10.6 us
    all_gather x1, blocking collectives, carried_in(): gathered = lax.all_gather(part, axis)  9.72 us
    slice x4, local copies, waits for them, and re-layouts, march_slabs(): tails = passed_along((dens_ext[:, :, :1], lit_ext[:, :, :1]), 'light', -1)  8.64 us
    all_to_all x1, starting transfers between devices, local(): lax.all_to_all(lit_cam, 'light', split_axis=0, concat_axis=2, tiled=True)  6.94 us
    all_to_all x1, starting transfers between devices, march_slabs(): lax.all_to_all(total[None], 'screen', split_axis=1, concat_axis=0, tiled=...  6.67 us
  transfers between devices with their start and end apart: 8, of which 4 were waited for; matrix products, arithmetic and copies ran while one was open for 24% of the time, Pallas kernels for 0%

commit v1 on v0

--- a/solution.py
+++ b/solution.py
@@ -4,6 +4,29 @@
 from jax.sharding import PartitionSpec as P
 
 BRICK = 16
+
+
+def cut_along(array, dim, size):
+    lengths = array.shape
+    blocks = array.reshape(*lengths[:dim], size, lengths[dim] // size, *lengths[dim + 1 :])
+    return jnp.moveaxis(blocks, dim, 0)
+
+
+def in_order(blocks, dim):
+    shape = list(blocks.shape[1:])
+    shape[dim] *= blocks.shape[0]
+    return jnp.moveaxis(blocks, 0, dim).reshape(shape)
+
+
+def exchange_in_pairs(array, axis, split_dim, concat_dim):
+    size, place = (lax.axis_size(axis), lax.axis_index(axis))
+    tiles = cut_along(array, split_dim, size)
+    gathered = [tiles[place]]
+    for step in range(1, size):
+        sent = tiles[place ^ step]
+        gathered.append(lax.ppermute(sent, axis, [(i, i ^ step) for i in range(size)]))
+    tiles = jnp.stack(gathered)[place ^ jnp.arange(size)]
+    return in_order(tiles, concat_dim)
 
 
 def passed_along(value, axis, by):
@@ -119,7 +142,7 @@
     incoming = lax.dynamic_slice_in_dim(light_in, screen_idx * slab_b, slab_b, 0)
     lit = albedo * incoming[:, :, None] * jnp.exp(-(local_depth + before[:, :, None]))
     lit_cam = lax.all_to_all(lit, "screen", split_axis=1, concat_axis=0, tiled=True)
-    lit_cam = lax.all_to_all(lit_cam, "light", split_axis=0, concat_axis=2, tiled=True)
+    lit_cam = exchange_in_pairs(lit_cam, "light", 0, 2)
     picture, passing = march_slabs(masked, lit, phase, fractions)
     return (picture, passing, lit_cam)
 

time: 197 us -> 169 us (0.86)
  waiting for transfers between devices: 73.3 us -> 17.3 us
  starting transfers between devices: 26.8 us -> 52.1 us
  other arithmetic: 30.4 us -> 33.5 us
    all_to_all x1, waiting for transfers between devices: 42.7 us -> 0.01 us  [local(): lax.all_to_all(lit, 'screen', split_axis=1, concat_axis=0, tiled=True)]
    all_to_all x1, starting transfers between devices: 6.67 us -> 31 us  [march_slabs(): lax.all_to_all(total[None], 'screen', split_axis=1, concat_axis=0, tiled=...]
    all_to_all x1 -> x0, waiting for transfers between devices: 23.3 us -> none  [local(): lax.all_to_all(lit_cam, 'light', split_axis=0, concat_axis=2, tiled=True)]
    ppermute x0 -> x3, waiting for transfers between devices: none -> 11.2 us  [exchange_in_pairs(): lax.ppermute(sent, axis, [(i, i ^ step) for i in range(size)])]
    all_to_all x1 -> x0, starting transfers between devices: 6.94 us -> none  [local(): lax.all_to_all(lit_cam, 'light', split_axis=0, concat_axis=2, tiled=True)]
    ppermute x0 -> x3, starting transfers between devices: none -> 4.85 us  [exchange_in_pairs(): lax.ppermute(sent, axis, [(i, i ^ step) for i in range(size)])]
    all_to_all x1, waiting for transfers between devices: 4.2 us -> 0.01 us  [march_slabs(): lax.all_to_all(total[None], 'screen', split_axis=1, concat_axis=0, tiled=...]
    reshape x0 -> x1, local copies, waits for them, and re-layouts: none -> 3.2 us  [in_order(): return jnp.moveaxis(blocks, 0, dim).reshape(shape)]
  transfers between devices with their start and end apart: 8 -> 10, of which waited for: 4 -> 3; matrix products, arithmetic and copies ran while one was open for 24% -> 43% of each run, Pallas kernels for 0% -> 0%
where the time goes in v1:
time: 169 us; the launch traced here: 168 us
  starting transfers between devices  52.1 us (31%)
  local copies, waits for them, and re-layouts  47.2 us (28%)
  other arithmetic  33.5 us (20%)
  waiting for transfers between devices  17.3 us (10%)
  blocking collectives  9.72 us (6%)
  matrix products  7 us (4%)
    all_to_all x1, starting transfers between devices, march_slabs(): lax.all_to_all(total[None], 'screen', split_axis=1, concat_axis=0, tiled=...  31 us
    add x1, other arithmetic, resample(): mixed = near + light_w * (further - near)  11.9 us
    ppermute x3, waiting for transfers between devices, exchange_in_pairs(): lax.ppermute(sent, axis, [(i, i ^ step) for i in range(size)])  11.2 us
    all_gather x1, blocking collectives, carried_in(): gathered = lax.all_gather(part, axis)  9.72 us
    slice x4, local copies, waits for them, and re-layouts, march_slabs(): tails = passed_along((dens_ext[:, :, :1], lit_ext[:, :, :1]), 'light', -1)  8.66 us
    reshape x1, local copies, waits for them, and re-layouts, local(): density.reshape(bricks_b, BRICK, bricks_a, BRICK, bricks_l, BRICK)  8.5 us
    all_to_all x1, waiting for transfers between devices, march_slabs(): lax.all_to_all(part[None], 'screen', split_axis=1, concat_axis=0, tiled=T...  6.1 us
    all_to_all x1, starting transfers between devices, local(): lax.all_to_all(lit, 'screen', split_axis=1, concat_axis=0, tiled=True)  5.75 us
  transfers between devices with their start and end apart: 10, of which 3 were waited for; matrix products, arithmetic and copies ran while one was open for 43% of the time, Pallas kernels for 0%

profile of v1, /device:TPU:0, one launch (start us, length us, event | category | flops | bytes accessed | tf_op | source)
XLA Modules:
  0.0 167.9 jit_solution(17715180105733979930)
XLA Ops:
  0.7 0.7 convert_bitcast_fusion
  1.9 2.2 %fusion.36 = (f32[16,256]{1,0:T(8,128)S(1)}, f32[16,256,128]{2,1,0:T(8,128)S(1)}) fusion(f32[16,256,128]{2,1,0:T(8,128)} %param.8, f32[256,128]{1,0:T(8,128)S(1)} %mul.121), kind=kLoop, calls=%fused_computation.71 | loop fusion | flops 1044480 | bytes 4341760 | tf_op jit(solution)/shard_map/reduce_sum | solution.py:58
  4.2 9.7 %all-gather = f32[64,256]{1,0:T(8,128)S(1)} all-gather(f32[16,256]{1,0:T(8,128)S(1)} %get-tuple-element.35), channel_id=2, replica_groups=mesh['light'=4,'screen'=8] {'light'}, dimensions={0}, use_global_device_ids=true | all-gather | bytes 81920 | tf_op jit(solution)/shard_map/all_gather | solution.py:40
  13.9 0.7 constant_dynamic-slice_fusion.1
  14.6 3.8 %exponential_multiply_fusion = f32[16,256,128]{2,1,0:T(8,128)S(1)} fusion(f32[16,256,128]{2,1,0:T(8,128)} %param.9, f32[16,256,128]{2,1,0:T(8,128)S(1)} %get-tuple-element.36, f32[16,256]{1,0:T(8,128)S(1)} %get-tuple-element.26, f32[16,256]{1,0:T(8,128)S(1)} %sub.66, f32[16,256]{1,0:T(8,128)S(1)} %constant_dynamic-slice_fusion.1), kind=kOutput, calls=%fused_computation.44 | convolution fusion | flops 807944192 | bytes 6340608 | tf_op jit(solution)/shard_map/dot_general | solution.py:57
  18.5 1.3 collective-permute-start.2
  19.8 2.5 %copy.36 = f32[16,256,128]{2,0,1:T(8,128)} copy(f32[16,256,128]{2,1,0:T(8,128)S(1)} %exponential_multiply_fusion) | data formatting | bytes 4194304 | tf_op jit(solution)/shard_map/mul | solution.py:143
  22.4 5.7 %all-to-all-start.2 = ((f32[16,256,128]{2,0,1:T(8,128)}), f32[16,256,128]{2,0,1:T(8,128)}, u32[]{:S(2)}, u32[]{:S(2)}) async-start(f32[16,256,128]{2,0,1:T(8,128)} %copy.36), calls=%async_computation.2 | async-start | bytes 4194304 | tf_op jit(solution)/shard_map/all_to_all | solution.py:144
  28.1 8.5 %reshape.105 = f32[1,16,16,16,8,16]{5,4,3,2,1,0:T(8,128)} reshape(f32[16,256,128]{2,1,0:T(8,128)S(1)} %copy-done.8) | data formatting | bytes 4194304 | tf_op jit(solution)/shard_map/reshape | solution.py:135
  36.6 1.9 %slice_multiply_fusion = f32[1,2,16,16,8,16]{5,4,3,2,1,0:T(8,128)S(1)} fusion(f32[1,16,16,16,8,16]{5,4,3,2,1,0:T(8,128)} %reshape.105, f32[16,8]{1,0:T(8,128)S(1)} %copy.28), kind=kLoop, calls=%fused_computation.42 | loop fusion | flops 65536 | bytes 524800 | tf_op jit(solution)/shard_map/mul | solution.py:135
  38.5 1.3 slice.74
  39.8 1.3 collective-permute-start
  41.1 0.7 fusion.27
  41.9 1.0 fusion.39
  42.9 1.7 %pad_maximum_fusion.1 = f32[18,256,128]{2,1,0:T(8,128)S(1)} fusion(f32[2,256,128]{2,1,0:T(8,128)S(1)} %collective-permute-done.2, f32[16,256,128]{2,1,0:T(8,128)} %copy-done.4), kind=kLoop, calls=%fused_computation.9 | loop fusion | flops 589824 | bytes 4718592 | tf_op jit(solution)/shard_map/concatenate | solution.py:117
  44.6 1.6 pad_slice_fusion.3
  46.3 2.7 %copy.33 = f32[18,258,1]{1,2,0:T(1,128)S(1)} copy(f32[18,258,1]{2,1,0:T(8,128)} %pad_slice_fusion.3) | data formatting | bytes 37152 | tf_op jit(solution)/shard_map/slice | solution.py:118
  49.0 1.3 collective-permute-start.3
  50.3 1.7 %pad_maximum_fusion = f32[18,256,128]{2,1,0:T(8,128)S(1)} fusion(f32[2,256,128]{2,1,0:T(8,128)S(1)} %collective-permute-done, f32[16,256,128]{2,1,0:T(8,128)} %copy-done.6), kind=kLoop, calls=%fused_computation.7 | loop fusion | flops 589824 | bytes 4718592 | tf_op jit(solution)/shard_map/concatenate | solution.py:116
  52.0 1.5 copy-done.2
  53.5 1.6 pad_slice_fusion.5
  55.1 2.7 %copy.30 = f32[18,258,1]{1,2,0:T(1,128)S(1)} copy(f32[18,258,1]{2,1,0:T(8,128)} %pad_slice_fusion.5) | data formatting | bytes 37152 | tf_op jit(solution)/shard_map/slice | solution.py:118
  57.8 1.6 collective-permute-start.1
  59.4 2.2 %pad_slice_fusion.2 = f32[18,256,127]{2,1,0:T(8,128)} fusion(f32[18,256,128]{2,1,0:T(8,128)S(1)} %pad_maximum_fusion.1), kind=kLoop, calls=%fused_computation.26 | loop fusion | bytes 4700160 | tf_op jit(solution)/shard_map/slice | solution.py:88
  61.6 2.1 %pad_slice_fusion.4 = f32[18,256,127]{2,1,0:T(8,128)} fusion(f32[18,256,128]{2,1,0:T(8,128)S(1)} %copy-done.3), kind=kLoop, calls=%fused_computation.28 | loop fusion | bytes 4700160 | tf_op jit(solution)/shard_map/slice | solution.py:88
  63.7 2.1 %fusion.3 = f32[18,256,127]{2,1,0:T(8,128)} fusion(f32[2,256,128]{2,1,0:T(8,128)S(1)} %collective-permute-done.2, f32[16,256,128]{2,1,0:T(8,128)S(1)} %copy-done.5), kind=kLoop, calls=%fused_computation.10 | loop fusion | flops 585216 | bytes 4700160 | tf_op jit(solution)/shard_map/concatenate | solution.py:117
  65.8 2.1 %fusion.4 = f32[18,256,127]{2,1,0:T(8,128)} fusion(f32[2,256,128]{2,1,0:T(8,128)S(1)} %collective-permute-done, f32[16,256,128]{2,1,0:T(8,128)S(1)} %copy-done.7), kind=kLoop, calls=%fused_computation.11 | loop fusion | flops 585216 | bytes 4700160 | tf_op jit(solution)/shard_map/concatenate | solution.py:116
  68.1 2.1 %copy.35 = f32[18,256,1]{2,1,0:T(8,128)} copy(f32[18,256,1]{1,2,0:T(1,128)S(1)} %get-tuple-element.48) | data formatting | bytes 36864 | tf_op jit(solution)/shard_map/slice | solution.py:86
  70.2 2.2 %copy.34 = f32[18,256,1]{2,1,0:T(8,128)} copy(f32[18,256,1]{1,2,0:T(1,128)S(1)} %get-tuple-element.49) | data formatting | bytes 36864 | tf_op jit(solution)/shard_map/slice | solution.py:85
  72.5 2.2 %copy.32 = f32[18,256,1]{2,1,0:T(8,128)} copy(f32[18,256,1]{1,2,0:T(1,128)S(1)} %get-tuple-element.50) | data formatting | bytes 36864 | tf_op jit(solution)/shard_map/slice | solution.py:86
  74.6 2.2 %copy.31 = f32[18,256,1]{2,1,0:T(8,128)} copy(f32[18,256,1]{1,2,0:T(1,128)S(1)} %get-tuple-element.51) | data formatting | bytes 36864 | tf_op jit(solution)/shard_map/slice | solution.py:85
  76.8 11.9 %fusion.14 = (f32[18,256,128]{2,1,0:T(8,128)}, f32[18,256,128]{2,1,0:T(8,128)S(1)}) fusion(f32[18,256,1]{2,1,0:T(8,128)} %copy.34, f32[18,256,127]{2,1,0:T(8,128)} %fusion.3, f32[18,256,1]{2,1,0:T(8,128)} %copy.35, f32[18,256,127]{2,1,0:T(8,128)} %pad_slice_fusion.2, f32[18,256,128]{2,1,0:T(8,128)S(1)} %pad_maximum_fusion.1, f32[256,128]{1,0:T(8,128)S(1)} %bitcast.83, ...), kind=kLoop, calls=%fused_computation.25 | loop fusion | flops 12976128 | bytes 19136512 | tf_op jit(solution)/shard_map/add | solution.py:94
  88.7 1.1 fusion.37
  89.7 0.9 subtract_bitcast_fusion
  90.6 2.5 %fusion.24 = f32[2,8,256,128]{3,1,2,0:T(8,128)S(1)} fusion(f32[2,8,256,128]{3,2,1,0:T(8,128)S(1)} %bitcast.77, f32[32768]{0:T(1024)S(1)} %subtract_bitcast_fusion), kind=kOutput, calls=%fused_computation.47 | convolution fusion | flops 101712128 | bytes 4325376 | tf_op jit(solution)/shard_map/ij,bjr->bir/dot_general | solution.py:70
  93.1 1.7 %copy.43 = f32[2,8,256,128]{3,2,1,0:T(8,128)} copy(f32[2,8,256,128]{3,1,2,0:T(8,128)S(1)} %fusion.24) | data formatting | bytes 4194304
  94.8 31.0 %all-to-all-start = ((f32[1,256,128]{2,0,1:T(1,128)}), f32[1,256,128]{2,0,1:T(1,128)S(1)}, u32[]{:S(2)}, u32[]{:S(2)}) async-start(f32[1,256,128]{2,0,1:T(1,128)} %bitcast.7), calls=%async_computation | async-start | bytes 262144 | tf_op jit(solution)/shard_map/all_to_all | solution.py:126
  125.8 4.3 %fusion.16 = f32[256,128]{1,0:T(8,128)} fusion(f32[2,8,256,128]{3,2,1,0:T(8,128)} %copy.43, f32[18,256,128]{2,1,0:T(8,128)} %get-tuple-element.46, f32[16,256,128]{2,1,0:T(8,128)S(1)} %get-tuple-element.38, f32[256,128]{1,0:T(8,128)S(1)} %bitcast.82), kind=kLoop, calls=%fused_computation.32 | loop fusion | flops 4161536 | bytes 8650752 | tf_op jit(solution)/shard_map/reduce_sum | solution.py:102
  130.1 2.2 %copy.38 = f32[8,16,32,128]{3,2,1,0:T(8,128)S(1)} copy(f32[8,16,32,128]{3,1,2,0:T(8,128)} %bitcast.18) | data formatting | bytes 4194304 | tf_op jit(solution)/shard_map/all_to_all | solution.py:144
  132.6 3.4 %collective-permute-start.6 = (f32[32,32,128]{2,1,0:T(8,128)S(1)}, f32[32,32,128]{2,1,0:T(8,128)S(1)}, u32[]{:S(2)}, u32[]{:S(2)}) collective-permute-start(f32[32,32,128]{2,1,0:T(8,128)S(1)} %get-tuple-element.40), channel_id=1, source_target_pairs={{0,24},{8,16},{16,8},{24,0},{1,25},{9,17},{17,9},{25,1},{2,26},{10... | collective-permute-start | bytes 1572872 | tf_op jit(solution)/shard_map/ppermute | solution.py:27
  136.4 1.0 collective-permute-start.4
  137.4 5.1 %all-to-all-start.1 = ((f32[1,256,128]{2,0,1:T(1,128)}), f32[1,256,128]{2,0,1:T(1,128)S(1)}, u32[]{:S(2)}, u32[]{:S(2)}) async-start(f32[1,256,128]{2,0,1:T(1,128)} %bitcast.14), calls=%async_computation.1 | async-start | bytes 262144 | tf_op jit(solution)/shard_map/all_to_all | solution.py:125
  143.2 6.1 %all-to-all-done.1 = f32[1,256,128]{2,0,1:T(1,128)S(1)} async-done(((f32[1,256,128]{2,0,1:T(1,128)}), f32[1,256,128]{2,0,1:T(1,128)S(1)}, u32[]{:S(2)}, u32[]{:S(2)}) %all-to-all-start.1) | async-done | bytes 131104 | tf_op jit(solution)/shard_map/all_to_all | solution.py:125
  149.9 10.0 %collective-permute-done.5 = f32[32,32,128]{2,1,0:T(8,128)} collective-permute-done((f32[32,32,128]{2,1,0:T(8,128)S(1)}, f32[32,32,128]{2,1,0:T(8,128)}, u32[]{:S(2)}, u32[]{:S(2)}) %collective-permute-start.5) | collective-permute-done | bytes 524320 | tf_op jit(solution)/shard_map/ppermute | solution.py:27
  159.9 1.2 collective-permute-done.4
  161.1 1.5 pad_maximum_fusion.4
  162.6 2.0 %gather_fusion = f32[4,32,32,128]{3,2,1,0:T(8,128)} fusion(f32[4,32,32,128]{3,2,1,0:T(8,128)S(1)} %pad_maximum_fusion.4, s32[1024]{0:T(1024)S(1)} %pad_clamp_fusion), kind=kCustom, calls=%fused_computation | custom fusion | bytes 4194320 | tf_op jit(solution)/shard_map/gather | solution.py:28
  164.7 3.2 %copy_bitcast_fusion = f32[32,32,512]{2,1,0:T(8,128)} fusion(f32[4,32,32,128]{3,2,1,0:T(8,128)} %gather_fusion), kind=kLoop, calls=%fused_computation.35 | loop fusion | bytes 4194304 | tf_op jit(solution)/shard_map/reshape | solution.py:18
  (49 shorter events, 2.8 us)
Async XLA Ops:
  0.6 40.5 %copy-start = (s32[256,512]{1,0:T(8,128)S(1)}, s32[256,512]{1,0:T(8,128)}, u32[]{:S(2)}) copy-start(s32[256,512]{1,0:T(8,128)} %param.12) | copy-start | bytes 1572868
  4.1 14.3 %copy-start.6 = (f32[16,256,128]{2,1,0:T(8,128)}, f32[16,256,128]{2,1,0:T(8,128)S(1)}, u32[]{:S(2)}) copy-start(f32[16,256,128]{2,1,0:T(8,128)S(1)} %get-tuple-element.36) | copy-start | bytes 6291460
  18.5 1.3 copy-start.4
  18.5 24.3 %collective-permute-start.2 = (f32[2,256,128]{2,1,0:T(8,128)S(1)}, f32[2,256,128]{2,1,0:T(8,128)S(1)}, u32[]{:S(2)}, u32[]{:S(2)}) collective-permute-start(f32[2,256,128]{2,1,0:T(8,128)S(1)} %slice.107), channel_id=1, source_target_pairs={{1,0},{2,1},{3,2},{4,3},{5,4},{6,5},{7,6},{9,8},{10,9},{11,10},{12... | collective-permute-start | bytes 786440 | tf_op jit(solution)/shard_map/ppermute | solution.py:35
  22.4 5.8 %copy-start.8 = (f32[16,256,128]{2,1,0:T(8,128)S(1)}, f32[16,256,128]{2,1,0:T(8,128)}, u32[]{:S(2)}) copy-start(f32[16,256,128]{2,1,0:T(8,128)} %param.8) | copy-start | bytes 6291460
  22.4 72.5 %all-to-all-start.2 = ((f32[16,256,128]{2,0,1:T(8,128)}), f32[16,256,128]{2,0,1:T(8,128)}, u32[]{:S(2)}, u32[]{:S(2)}) async-start(f32[16,256,128]{2,0,1:T(8,128)} %copy.36), calls=%async_computation.2 | async-start | bytes 4194304 | tf_op jit(solution)/shard_map/all_to_all | solution.py:144
  38.5 2.6 %copy-start.12 = (f32[3,16]{1,0:T(4,128)S(1)}, f32[3,16]{1,0:T(4,128)}, u32[]{:S(2)}) copy-start(f32[3,16]{1,0:T(4,128)} %param.13) | copy-start | bytes 580
  39.8 10.5 %collective-permute-start = (f32[2,256,128]{2,1,0:T(8,128)}, f32[2,256,128]{2,1,0:T(8,128)S(1)}, u32[]{:S(2)}, u32[]{:S(2)}) collective-permute-start(f32[2,256,128]{2,1,0:T(8,128)} %slice.74), channel_id=1, source_target_pairs={{1,0},{2,1},{3,2},{4,3},{5,4},{6,5},{7,6},{9,8},{10,9},{11,10},{12... | collective-permute-start | bytes 786440 | tf_op jit(solution)/shard_map/ppermute | solution.py:35
  49.0 19.0 %collective-permute-start.3 = (f32[18,258,1]{1,2,0:T(1,128)S(1)}, f32[18,258,1]{1,2,0:T(1,128)S(1)}, u32[]{:S(2)}, u32[]{:S(2)}) collective-permute-start(f32[18,258,1]{1,2,0:T(1,128)S(1)} %copy.33), channel_id=1, source_target_pairs={{8,0},{16,8},{24,16},{9,1},{17,9},{25,17},{10,2},{18,10},{26,18},{... | collective-permute-start | bytes 55736 | tf_op jit(solution)/shard_map/ppermute | solution.py:35
  52.0 1.5 copy-start.2
  57.8 3.8 %copy-start.3 = (f32[18,256,128]{2,1,0:T(8,128)S(1)}, f32[18,256,128]{2,1,0:T(8,128)}, u32[]{:S(2)}) copy-start(f32[18,256,128]{2,1,0:T(8,128)} %copy-done.2) | copy-start | bytes 7077892
  57.8 14.5 %collective-permute-start.1 = (f32[18,258,1]{1,2,0:T(1,128)S(1)}, f32[18,258,1]{1,2,0:T(1,128)S(1)}, u32[]{:S(2)}, u32[]{:S(2)}) collective-permute-start(f32[18,258,1]{1,2,0:T(1,128)S(1)} %copy.30), channel_id=1, source_target_pairs={{8,0},{16,8},{24,16},{9,1},{17,9},{25,17},{10,2},{18,10},{26,18},{... | collective-permute-start | bytes 55736 | tf_op jit(solution)/shard_map/ppermute | solution.py:35
  61.6 2.1 %copy-start.5 = (f32[16,256,128]{2,1,0:T(8,128)S(1)}, f32[16,256,128]{2,1,0:T(8,128)}, u32[]{:S(2)}) copy-start(f32[16,256,128]{2,1,0:T(8,128)} %copy-done.4) | copy-start | bytes 6291460
  63.7 2.1 %copy-start.7 = (f32[16,256,128]{2,1,0:T(8,128)S(1)}, f32[16,256,128]{2,1,0:T(8,128)}, u32[]{:S(2)}) copy-start(f32[16,256,128]{2,1,0:T(8,128)} %copy-done.6) | copy-start | bytes 6291460
  72.4 4.4 %copy-start.9 = (f32[1,256,128]{2,0,1:T(1,128)S(1)}, f32[1,256,128]{2,0,1:T(1,128)}, u32[]{:S(2)}) copy-start(f32[1,256,128]{2,0,1:T(1,128)} %get-tuple-element.44) | copy-start | bytes 393220
  72.4 4.4 %copy-start.10 = (f32[1,256,128]{2,0,1:T(1,128)S(1)}, f32[1,256,128]{2,0,1:T(1,128)}, u32[]{:S(2)}) copy-start(f32[1,256,128]{2,0,1:T(1,128)} %get-tuple-element.45) | copy-start | bytes 393220
  94.8 42.6 %all-to-all-start = ((f32[1,256,128]{2,0,1:T(1,128)}), f32[1,256,128]{2,0,1:T(1,128)S(1)}, u32[]{:S(2)}, u32[]{:S(2)}) async-start(f32[1,256,128]{2,0,1:T(1,128)} %bitcast.7), calls=%async_computation | async-start | bytes 262144 | tf_op jit(solution)/shard_map/all_to_all | solution.py:126
  132.6 17.3 %collective-permute-start.6 = (f32[32,32,128]{2,1,0:T(8,128)S(1)}, f32[32,32,128]{2,1,0:T(8,128)S(1)}, u32[]{:S(2)}, u32[]{:S(2)}) collective-permute-start(f32[32,32,128]{2,1,0:T(8,128)S(1)} %get-tuple-element.40), channel_id=1, source_target_pairs={{0,24},{8,16},{16,8},{24,0},{1,25},{9,17},{17,9},{25,1},{2,26},{10... | collective-permute-start | bytes 1572872 | tf_op jit(solution)/shard_map/ppermute | solution.py:27
  136.0 23.9 %collective-permute-start.5 = (f32[32,32,128]{2,1,0:T(8,128)S(1)}, f32[32,32,128]{2,1,0:T(8,128)}, u32[]{:S(2)}, u32[]{:S(2)}) collective-permute-start(f32[32,32,128]{2,1,0:T(8,128)S(1)} %get-tuple-element.41), channel_id=1, source_target_pairs={{0,16},{8,24},{16,0},{24,8},{1,17},{9,25},{17,1},{25,9},{2,18},{10... | collective-permute-start | bytes 1572872 | tf_op jit(solution)/shard_map/ppermute | solution.py:27
  136.4 24.6 %collective-permute-start.4 = (f32[32,32,128]{2,1,0:T(8,128)S(1)}, f32[32,32,128]{2,1,0:T(8,128)}, u32[]{:S(2)}, u32[]{:S(2)}) collective-permute-start(f32[32,32,128]{2,1,0:T(8,128)S(1)} %get-tuple-element.42), channel_id=1, source_target_pairs={{0,8},{8,0},{16,24},{24,16},{1,9},{9,1},{17,25},{25,17},{2,10},{10... | collective-permute-start | bytes 1572872 | tf_op jit(solution)/shard_map/ppermute | solution.py:27
  137.4 11.8 %all-to-all-start.1 = ((f32[1,256,128]{2,0,1:T(1,128)}), f32[1,256,128]{2,0,1:T(1,128)S(1)}, u32[]{:S(2)}, u32[]{:S(2)}) async-start(f32[1,256,128]{2,0,1:T(1,128)} %bitcast.14), calls=%async_computation.1 | async-start | bytes 262144 | tf_op jit(solution)/shard_map/all_to_all | solution.py:125
  149.9 11.2 %copy-start.11 = (f32[32,32,128]{2,1,0:T(8,128)}, f32[32,32,128]{2,1,0:T(8,128)S(1)}, u32[]{:S(2)}) copy-start(f32[32,32,128]{2,1,0:T(8,128)S(1)} %collective-permute-done.6) | copy-start | bytes 1572868
  162.6 5.2 %copy-start.1 = (s32[256,512]{1,0:T(8,128)S(1)}, s32[256,512]{1,0:T(8,128)}, u32[]{:S(2)}) copy-start(s32[256,512]{1,0:T(8,128)} %param.12) | copy-start | bytes 1572868
